TPU v7x, 32 devices: a whole 2x2x4 slice. The times are simulated.
32 devices in a mesh: groups: 2 (over y), pts: 4 (over z), cb: 4 (over x, core).
Axes of the slice: x: 2, y: 2, z: 4, core: 2. Of those that a mesh axis runs over, the one named last changes fastest.
Arguments:
- points: bfloat16 [16384, 768], P(('groups', 'pts')), parts along dimension 0, may hold values from -60 to 60
- code_one: int32 [16384], P(('groups', 'pts')), parts along dimension 0, may hold values from 0 to 2047
- code_two: int32 [16384], P(('groups', 'pts')), parts along dimension 0, may hold values from 0 to 2047
- cent_one: bfloat16 [4096, 768], P(('groups', 'cb')), parts along dimension 0, may hold values from -6 to 6
- cent_two: bfloat16 [4096, 768], P(('groups', 'cb')), parts along dimension 0, may hold values from -6 to 6
Outputs:
- new_one: bfloat16 [4096, 768], P(('groups', 'cb')), parts along dimension 0
- new_two: bfloat16 [4096, 768], P(('groups', 'cb')), parts along dimension 0
- distortion: float32 [4], P('groups'), parts along dimension 0
There are 2 independent parts, one for each index of `groups`. A program takes and returns all parts, laid end to end along the dimension named above; each array names one. Nothing has to cross between parts.
All inputs are finite; a program needn't handle non-finite values.
Results may differ from a plain program's by a relative error of at most 0.0014.
Values may be sent and summed in bfloat16 or wider, within the bound.
A program may use at most 64 MiB of HBM per device.

v0:
```python
import jax
import jax.numpy as jnp
from jax import lax
from jax.sharding import PartitionSpec as P


def nearest_local(data, cents):
    sq = jnp.sum(jnp.square(data.astype(jnp.float32)), axis=1)
    csq = jnp.sum(jnp.square(cents.astype(jnp.float32)), axis=1)
    cross = lax.dot_general(
        data, cents, (((1,), (1,)), ((), ())), preferred_element_type=jnp.float32
    )
    dist = sq[:, None] - 2.0 * cross + csq[None, :]
    local_min = jnp.min(dist, axis=1)
    best = lax.pmin(local_min, "cb")
    return jnp.sum(best)


def section_update(data, codes, cents):
    rows = cents.shape[0]
    first = lax.axis_index("cb") * rows
    labels = first + lax.broadcasted_iota(jnp.int32, (1, rows), 1)
    onehot = (codes[:, None] == labels).astype(jnp.bfloat16)
    sums = lax.dot_general(
        onehot, data, (((0,), (0,)), ((), ())), preferred_element_type=jnp.float32
    )
    counts = jnp.sum(onehot.astype(jnp.float32), axis=0)
    share_sums, share_counts = (
        lax.psum_scatter(sums, "pts", scatter_dimension=0, tiled=True),
        lax.psum_scatter(counts, "pts", scatter_dimension=0, tiled=True),
    )
    share_rows = share_sums.shape[0]
    old_rows = lax.dynamic_slice_in_dim(cents, lax.axis_index("pts") * share_rows, share_rows, 0)
    return ((share_sums + old_rows.astype(jnp.float32)) / (share_counts + 1.0)[:, None]).astype(
        jnp.bfloat16
    )


def section_total(value):
    return lax.psum(value, "pts")


def local(points, code_one, code_two, cent_one, cent_two):
    rows = cent_one.shape[0]
    width = points.shape[1]
    npts = lax.axis_size("pts")
    ncb = lax.axis_size("cb")
    first = lax.axis_index("cb") * rows
    first_local = nearest_local(points, cent_one)
    updated_one = section_update(points, code_one, cent_one)
    gathered = lax.all_gather(updated_one, ("pts", "cb"), axis=0, tiled=True)
    share_rows = updated_one.shape[0]
    codebook = jnp.swapaxes(gathered.reshape(npts, ncb, share_rows, width), 0, 1).reshape(
        rows * ncb, width
    )
    new_one = lax.dynamic_slice_in_dim(codebook, first, rows, 0)
    looked = jnp.take(codebook, code_one, axis=0)
    residual = (points.astype(jnp.float32) - looked.astype(jnp.float32)).astype(jnp.bfloat16)
    updated_two = section_update(residual, code_two, cent_two)
    new_two = lax.all_gather(updated_two, "pts", axis=0, tiled=True)
    second_local = nearest_local(residual, cent_two)
    first_sum = section_total(first_local)
    second_sum = section_total(second_local)
    scale = jnp.float32(points.shape[0] * npts * width)
    distortion = jnp.stack([first_sum, second_sum]) / scale
    return (new_one, new_two, distortion)


def solution(mesh):
    return jax.shard_map(
        local,
        mesh=mesh,
        in_specs=(
            P(("groups", "pts"), None),
            P(("groups", "pts")),
            P(("groups", "pts")),
            P(("groups", "cb"), None),
            P(("groups", "cb"), None),
        ),
        out_specs=(P(("groups", "cb"), None), P(("groups", "cb"), None), P("groups")),
        check_vma=False,
    )
```

profile of v0, /device:TPU:0, one launch (start us, length us, event | category | flops | bytes accessed | tf_op | source)
XLA Modules:
  0.0 180.3 jit_solution(905735486691300784)
XLA Ops:
  7.3 5.2 %fusion.4 = f32[512,768]{1,0:T(8,128)} fusion(bf16[2048,768]{1,0:T(8,128)(2,1)} %param.5, s32[512]{0:T(512)S(1)} %iota_add_fusion, s32[2048]{0:T(1024)} %param.6), kind=kOutput, calls=%fused_computation.10 | convolution fusion | flops 1611661312 | bytes 4728832 | tf_op jit(solution)/shard_map/dot_general | solution.py:24
  13.8 1.2 convert_reduce_fusion
  15.1 13.9 %all-reduce = f32[512]{0:T(512)S(1)} all-reduce(f32[512]{0:T(512)S(1)} %get-tuple-element.4), channel_id=3, replica_groups=mesh['groups'=2,'pts'=4,'cb'=4] {'pts'}, use_global_device_ids=true, to_apply=%region_2.0.clone | all-reduce | flops 512 | bytes 4096
  29.0 21.9 %reduce-scatter.3.cloned.1.call-done = f32[128,768]{1,0:T(8,128)} async-done(((f32[512,768]{1,0:T(8,128)}), f32[128,768]{1,0:T(8,128)}) %reduce-scatter.3.cloned.1.call-update) | async-done | bytes 393232 | tf_op jit(solution)/shard_map/reduce_scatter | solution.py:29
  50.9 1.8 %divide_convert_fusion.1 = bf16[128,768]{1,0:T(8,128)(2,1)} fusion(f32[128,768]{1,0:T(8,128)} %reduce-scatter.3.cloned.1.call-done, f32[128]{0:T(128)S(1)} %dynamic-slice_add_fusion.1, bf16[512,768]{1,0:T(8,128)(2,1)} %param.8, s32[]{:T(128)S(6)} %select_n.16), kind=kLoop, calls=%fused_computation.23 | loop fusion | flops 393216 | bytes 786948 | tf_op jit(solution)/shard_map/convert_element_type | solution.py:34
  52.8 45.4 %all-gather.2.cloned.1.call-done = bf16[2048,768]{1,0:T(8,128)(2,1)} async-done(((bf16[128,768]{1,0:T(8,128)(2,1)}), bf16[2048,768]{1,0:T(8,128)(2,1)}) %all-gather.2.cloned.1.call-update) | async-done | bytes 3145744 | tf_op jit(solution)/shard_map/all_gather | solution.py:51
  98.2 2.1 %copy.10 = bf16[4,4,128,768]{3,2,1,0:T(8,128)(2,1)S(1)} copy(bf16[4,4,128,768]{3,2,0,1:T(8,128)(2,1)} %bitcast.15) | data formatting | bytes 6291456 | tf_op jit(solution)/shard_map/transpose | solution.py:53
  100.3 9.4 %gather_fusion = bf16[2048,768]{1,0:T(8,128)(2,1)} fusion(bf16[2048,768]{1,0:T(8,128)(2,1)S(1)} %bitcast.13, s32[2048]{0:T(1024)S(1)} %fusion.10), kind=kCustom, calls=%fused_computation | custom fusion | bytes 6299648 | tf_op jit(solution)/shard_map/jit(_take)/gather | solution.py:57
  109.7 4.3 %multiply_reduce_fusion = (f32[2048]{0:T(1024)S(1)}, bf16[2048,768]{1,0:T(8,128)(2,1)S(1)}, f32[2048]{0:T(1024)S(1)}) fusion(bf16[2048,768]{1,0:T(8,128)(2,1)} %gather_fusion, pred[2048]{0:T(1024)(128)(4,1)S(1)} %compare_and_fusion, bf16[2048,768]{1,0:T(8,128)(2,1)} %param.5), kind=kLoop, calls=%fused_computation.5 | loop fusion | flops 15724544 | bytes 9455616 | tf_op jit(solution)/shard_map/reduce_sum | solution.py:8
  114.0 1.7 copy-done.1
  115.7 3.3 %fusion.2 = f32[512,768]{1,0:T(8,128)} fusion(bf16[2048,768]{1,0:T(8,128)(2,1)S(1)} %get-tuple-element.11, s32[512]{0:T(512)S(1)} %iota_add_fusion, s32[2048]{0:T(1024)S(1)} %copy-done.4), kind=kOutput, calls=%fused_computation.7 | convolution fusion | flops 1611661312 | bytes 4728832 | tf_op jit(solution)/shard_map/dot_general | solution.py:24
  119.0 1.4 multiply_reduce_fusion.2
  120.4 1.4 multiply_reduce_fusion.1
  121.8 4.3 %add_reduce_fusion = f32[2048]{0:T(1024)S(1)} fusion(bf16[2048,768]{1,0:T(8,128)(2,1)} %copy-done.1, bf16[512,768]{1,0:T(8,128)(2,1)} %param.9, f32[512]{0:T(512)S(1)} %multiply_reduce_fusion.1, f32[2048]{0:T(1024)S(1)} %get-tuple-element.10), kind=kOutput, calls=%fused_computation.12 | convolution fusion | flops 1614804992 | bytes 3950592 | tf_op jit(solution)/shard_map/dot_general | solution.py:10
  126.2 1.8 %add_reduce_fusion.1 = f32[2048]{0:T(1024)S(1)} fusion(bf16[2048,768]{1,0:T(8,128)(2,1)S(1)} %copy-done, bf16[512,768]{1,0:T(8,128)(2,1)S(1)} %copy-done.2, f32[512]{0:T(512)S(1)} %multiply_reduce_fusion.2, f32[2048]{0:T(1024)S(1)} %get-tuple-element.12), kind=kOutput, calls=%fused_computation.13 | convolution fusion | flops 1614804992 | bytes 3950592 | tf_op jit(solution)/shard_map/dot_general | solution.py:10
  128.0 11.0 %all-reduce.3 = (f32[2048]{0:T(1024)S(1)}, f32[2048]{0:T(1024)S(1)}) all-reduce(f32[2048]{0:T(1024)S(1)} %add_reduce_fusion, f32[2048]{0:T(1024)S(1)} %add_reduce_fusion.1), channel_id=1, replica_groups=mesh['groups'=2,'pts'=4,'cb'=4] {'cb'}, use_global_device_ids=true, to_apply=%region_15.16 | all-reduce | flops 4096 | bytes 32768 | tf_op jit(solution)/shard_map/pmin | solution.py:15
  139.0 0.6 reduce_sum.79
  139.6 0.6 reduce_sum.76
  140.2 11.1 %all-reduce.2 = (f32[512]{0:T(512)S(1)}, f32[1]{0:T(128)}, f32[1]{0:T(128)}) all-reduce(f32[512]{0:T(512)S(1)} %get-tuple-element.3, f32[1]{0:T(128)} %bitcast.4, f32[1]{0:T(128)} %bitcast.3), channel_id=5, replica_groups=mesh['groups'=2,'pts'=4,'cb'=4] {'pts'}, use_global_device_ids=true, to_apply=%region_5.0.clone | all-reduce | flops 514 | bytes 4112
  151.4 1.9 %maximum_multiply_fusion = f32[2]{0:T(128)} fusion(f32[1]{0:T(128)} %get-tuple-element.6, f32[1]{0:T(128)} %get-tuple-element.7), kind=kLoop, calls=%fused_computation.29 | loop fusion | flops 4 | bytes 16 | tf_op jit(solution)/shard_map/div | solution.py:65
  153.2 0.9 constant_dynamic-slice_fusion
  154.2 1.1 divide_convert_fusion
  155.3 17.6 %all_gather.7 = bf16[512,768]{1,0:T(8,128)(2,1)S(1)} all-gather(bf16[128,768]{1,0:T(8,128)(2,1)S(1)} %divide_convert_fusion), channel_id=1, replica_groups=mesh['groups'=2,'pts'=4,'cb'=4] {'pts'}, dimensions={0}, use_global_device_ids=true | all-gather | bytes 983040 | tf_op jit(solution)/shard_map/all_gather | solution.py:60
  172.9 0.9 copy.12
  (24 shorter events, 1.0 us)
Async XLA Ops:
  7.2 43.7 %reduce-scatter.3.cloned.1.call-start = ((), (), s32[]{:S(2)}) async-start(), calls=%async_computation.2 | async-start | bytes 1966080 | tf_op jit(solution)/shard_map/reduce_scatter | solution.py:29
  7.2 5.3 %copy-start.5 = (u32[32]{0:T(128)S(1)}, u32[32]{0:T(128)}, u32[]{:S(2)}) copy-start(u32[32]{0:T(128)} %constant.42) | copy-start | bytes 388
  7.2 6.6 %copy-start.3 = (s32[2048]{0:T(1024)S(1)}, s32[2048]{0:T(1024)}, u32[]{:S(2)}) copy-start(s32[2048]{0:T(1024)} %param.6) | copy-start | bytes 24580
  7.3 6.6 %copy-start.4 = (s32[2048]{0:T(1024)S(1)}, s32[2048]{0:T(1024)}, u32[]{:S(2)}) copy-start(s32[2048]{0:T(1024)} %param.7) | copy-start | bytes 24580
  12.5 85.7 %all-gather.2.cloned.1.call-start = ((), (), s32[]{:S(2)}) async-start(), calls=%async_computation.3 | async-start | bytes 3342336 | tf_op jit(solution)/shard_map/all_gather | solution.py:51
  52.8 101.4 %reduce-scatter.5.cloned.1.call-start = ((), (), s32[]{:S(2)}) async-start(), calls=%async_computation.4 | async-start | bytes 1966080 | tf_op jit(solution)/shard_map/reduce_scatter | solution.py:29
  114.0 1.7 copy-start.1
  121.8 4.4 %copy-start = (bf16[2048,768]{1,0:T(8,128)(2,1)S(1)}, bf16[2048,768]{1,0:T(8,128)(2,1)}, u32[]{:S(2)}) copy-start(bf16[2048,768]{1,0:T(8,128)(2,1)} %param.5) | copy-start | bytes 9437188
  121.8 4.4 %copy-start.2 = (bf16[512,768]{1,0:T(8,128)(2,1)S(1)}, bf16[512,768]{1,0:T(8,128)(2,1)}, u32[]{:S(2)}) copy-start(bf16[512,768]{1,0:T(8,128)(2,1)} %param.8) | copy-start | bytes 2359300
Sparse Core Ops, SparseCore 0:
  12.6 38.2 reduce-scatter.2
  53.8 44.3 all-gather.1
  119.2 34.0 reduce-scatter.4
where the time goes:
time: 181 us; the launch traced here: 180 us
  waiting for transfers between devices  67.3 us (37%)
  blocking collectives  53.6 us (30%)
  local copies, waits for them, and re-layouts  15.6 us (9%)
  matrix products  14.7 us (8%)
  between operations  14.6 us (8%)
  other arithmetic  14.5 us (8%)
    all_gather x1, waiting for transfers between devices, local(): gathered = lax.all_gather(updated_one, ('pts', 'cb'), axis=0, tiled=True)  45.4 us
    unnamed x2, blocking collectives  25 us
    reduce_scatter x2, waiting for transfers between devices, section_update(): lax.psum_scatter(sums, 'pts', scatter_dimension=0, tiled=True)  21.9 us
    all_gather x1, blocking collectives, local(): new_two = lax.all_gather(updated_two, 'pts', axis=0, tiled=True)  17.6 us
    pmin x1, blocking collectives, nearest_local(): best = lax.pmin(local_min, 'cb')  11 us
    gather x1, local copies, waits for them, and re-layouts, local(): looked = jnp.take(codebook, code_one, axis=0)  9.38 us
    dot_general x2, matrix products, section_update(): lax.dot_general(onehot, data, (((0,), (0,)), ((), ())), preferred_element...  8.51 us
    dot_general x2, matrix products, nearest_local(): lax.dot_general(data, cents, (((1,), (1,)), ((), ())), preferred_element_...  6.18 us
  transfers between devices with their start and end apart: 3, of which 2 were waited for; matrix products, arithmetic and copies ran while one was open for 8% of the time, Pallas kernels for 0%

commit v1 on v0

--- a/solution.py
+++ b/solution.py
@@ -57,7 +57,12 @@
     looked = jnp.take(codebook, code_one, axis=0)
     residual = (points.astype(jnp.float32) - looked.astype(jnp.float32)).astype(jnp.bfloat16)
     updated_two = section_update(residual, code_two, cent_two)
-    new_two = lax.all_gather(updated_two, "pts", axis=0, tiled=True)
+    ring = [updated_two]
+    for hop in range(3):
+        ring.append(lax.ppermute(ring[-1], "pts", [(dev, (dev + 1) % 4) for dev in range(4)]))
+    new_two = jnp.roll(
+        jnp.concatenate(ring[::-1], axis=0), (lax.axis_index("pts") + 1) * ring[0].shape[0], axis=0
+    )
     second_local = nearest_local(residual, cent_two)
     first_sum = section_total(first_local)
     second_sum = section_total(second_local)

time: 181 us -> 188 us (1.039)
  waiting for transfers between devices: 67.3 us -> 89.5 us
  blocking collectives: 53.6 us -> 36 us
  local copies, waits for them, and re-layouts: 15.6 us -> 17.6 us
    ppermute x0 -> x3, waiting for transfers between devices: none -> 20.3 us  [local(): lax.ppermute(ring[-1], 'pts', [(dev, (dev + 1) % 4) for dev in range(4)])]
    all_gather x1 -> x0, blocking collectives: 17.6 us -> none  [local(): new_two = lax.all_gather(updated_two, 'pts', axis=0, tiled=True)]
    reduce_scatter x2, waiting for transfers between devices: 21.9 us -> 23.8 us  [section_update(): lax.psum_scatter(sums, 'pts', scatter_dimension=0, tiled=True)]
    unnamed x14 -> x20, local copies, waits for them, and re-layouts: 3.15 us -> 4.23 us
  transfers between devices with their start and end apart: 3 -> 6, of which waited for: 2 -> 6; matrix products, arithmetic and copies ran while one was open for 8% -> 8% of each run, Pallas kernels for 0% -> 0%
where the time goes in v1:
time: 188 us; the launch traced here: 187 us
  waiting for transfers between devices  89.5 us (48%)
  blocking collectives  36 us (19%)
  local copies, waits for them, and re-layouts  17.6 us (9%)
  matrix products  14.7 us (8%)
  between operations  14.6 us (8%)
  other arithmetic  14.5 us (8%)
    all_gather x1, waiting for transfers between devices, local(): gathered = lax.all_gather(updated_one, ('pts', 'cb'), axis=0, tiled=True)  45.4 us
    unnamed x2, blocking collectives  25 us
    reduce_scatter x2, waiting for transfers between devices, section_update(): lax.psum_scatter(sums, 'pts', scatter_dimension=0, tiled=True)  23.8 us
    ppermute x3, waiting for transfers between devices, local(): lax.ppermute(ring[-1], 'pts', [(dev, (dev + 1) % 4) for dev in range(4)])  20.3 us
    pmin x1, blocking collectives, nearest_local(): best = lax.pmin(local_min, 'cb')  11 us
    gather x1, local copies, waits for them, and re-layouts, local(): looked = jnp.take(codebook, code_one, axis=0)  9.38 us
    dot_general x2, matrix products, section_update(): lax.dot_general(onehot, data, (((0,), (0,)), ((), ())), preferred_element...  8.51 us
    dot_general x2, matrix products, nearest_local(): lax.dot_general(data, cents, (((1,), (1,)), ((), ())), preferred_element_...  6.18 us
  transfers between devices with their start and end apart: 6, of which 6 were waited for; matrix products, arithmetic and copies ran while one was open for 8% of the time, Pallas kernels for 0%

profile of v1, /device:TPU:0, one launch (start us, length us, event | category | flops | bytes accessed | tf_op | source)
XLA Modules:
  0.0 187.2 jit_solution(13931171131554714444)
XLA Ops:
  7.3 5.2 %fusion.4 = f32[512,768]{1,0:T(8,128)} fusion(bf16[2048,768]{1,0:T(8,128)(2,1)} %param.5, s32[512]{0:T(512)S(1)} %iota_add_fusion, s32[2048]{0:T(1024)} %param.6), kind=kOutput, calls=%fused_computation.10 | convolution fusion | flops 1611661312 | bytes 4728832 | tf_op jit(solution)/shard_map/dot_general | solution.py:24
  13.8 1.2 convert_reduce_fusion
  15.1 13.9 %all-reduce = f32[512]{0:T(512)S(1)} all-reduce(f32[512]{0:T(512)S(1)} %get-tuple-element.4), channel_id=3, replica_groups=mesh['groups'=2,'pts'=4,'cb'=4] {'pts'}, use_global_device_ids=true, to_apply=%region_2.0.clone | all-reduce | flops 512 | bytes 4096
  29.0 21.9 %reduce-scatter.3.cloned.1.call-done = f32[128,768]{1,0:T(8,128)} async-done(((f32[512,768]{1,0:T(8,128)}), f32[128,768]{1,0:T(8,128)}) %reduce-scatter.3.cloned.1.call-update) | async-done | bytes 393232 | tf_op jit(solution)/shard_map/reduce_scatter | solution.py:29
  50.9 1.8 divide_convert_fusion.1
  52.8 45.4 %all-gather.2.cloned.1.call-done = bf16[2048,768]{1,0:T(8,128)(2,1)} async-done(((bf16[128,768]{1,0:T(8,128)(2,1)}), bf16[2048,768]{1,0:T(8,128)(2,1)}) %all-gather.2.cloned.1.call-update) | async-done | bytes 3145744 | tf_op jit(solution)/shard_map/all_gather | solution.py:51
  98.2 2.1 %copy.10 = bf16[4,4,128,768]{3,2,1,0:T(8,128)(2,1)S(1)} copy(bf16[4,4,128,768]{3,2,0,1:T(8,128)(2,1)} %bitcast.15) | data formatting | bytes 6291456 | tf_op jit(solution)/shard_map/transpose | solution.py:53
  100.3 9.4 %gather_fusion = bf16[2048,768]{1,0:T(8,128)(2,1)} fusion(bf16[2048,768]{1,0:T(8,128)(2,1)S(1)} %bitcast.13, s32[2048]{0:T(1024)S(1)} %fusion.10), kind=kCustom, calls=%fused_computation | custom fusion | bytes 6299648 | tf_op jit(solution)/shard_map/jit(_take)/gather | solution.py:57
  109.7 4.3 %multiply_reduce_fusion = (f32[2048]{0:T(1024)S(1)}, bf16[2048,768]{1,0:T(8,128)(2,1)S(1)}, f32[2048]{0:T(1024)S(1)}) fusion(bf16[2048,768]{1,0:T(8,128)(2,1)} %gather_fusion, pred[2048]{0:T(1024)(128)(4,1)S(1)} %compare_and_fusion, bf16[2048,768]{1,0:T(8,128)(2,1)} %param.5), kind=kLoop, calls=%fused_computation.5 | loop fusion | flops 15724544 | bytes 9455616 | tf_op jit(solution)/shard_map/reduce_sum | solution.py:8
  114.0 1.7 copy-done.1
  115.7 3.3 %fusion.2 = f32[512,768]{1,0:T(8,128)} fusion(bf16[2048,768]{1,0:T(8,128)(2,1)S(1)} %get-tuple-element.11, s32[512]{0:T(512)S(1)} %iota_add_fusion, s32[2048]{0:T(1024)S(1)} %copy-done.4), kind=kOutput, calls=%fused_computation.7 | convolution fusion | flops 1611661312 | bytes 4728832 | tf_op jit(solution)/shard_map/dot_general | solution.py:24
  119.0 1.4 multiply_reduce_fusion.2
  120.4 1.4 multiply_reduce_fusion.1
  121.8 4.3 %add_reduce_fusion = f32[2048]{0:T(1024)S(1)} fusion(bf16[2048,768]{1,0:T(8,128)(2,1)} %copy-done.1, bf16[512,768]{1,0:T(8,128)(2,1)} %param.9, f32[512]{0:T(512)S(1)} %multiply_reduce_fusion.1, f32[2048]{0:T(1024)S(1)} %get-tuple-element.10), kind=kOutput, calls=%fused_computation.12 | convolution fusion | flops 1614804992 | bytes 3950592 | tf_op jit(solution)/shard_map/dot_general | solution.py:10
  126.2 1.8 add_reduce_fusion.1
  128.0 11.0 %all-reduce.3 = (f32[2048]{0:T(1024)S(1)}, f32[2048]{0:T(1024)S(1)}) all-reduce(f32[2048]{0:T(1024)S(1)} %add_reduce_fusion, f32[2048]{0:T(1024)S(1)} %add_reduce_fusion.1), channel_id=1, replica_groups=mesh['groups'=2,'pts'=4,'cb'=4] {'cb'}, use_global_device_ids=true, to_apply=%region_15.16 | all-reduce | flops 4096 | bytes 32768 | tf_op jit(solution)/shard_map/pmin | solution.py:15
  140.2 11.1 %all-reduce.2 = (f32[512]{0:T(512)S(1)}, f32[1]{0:T(128)}, f32[1]{0:T(128)}) all-reduce(f32[512]{0:T(512)S(1)} %get-tuple-element.3, f32[1]{0:T(128)} %bitcast.4, f32[1]{0:T(128)} %bitcast.3), channel_id=5, replica_groups=mesh['groups'=2,'pts'=4,'cb'=4] {'pts'}, use_global_device_ids=true, to_apply=%region_5.0.clone | all-reduce | flops 514 | bytes 4112
  151.4 1.9 %reduce-scatter.5.cloned.1.call-done = f32[128,768]{1,0:T(8,128)} async-done(((f32[512,768]{1,0:T(8,128)}), f32[128,768]{1,0:T(8,128)}) %reduce-scatter.5.cloned.1.call-update) | async-done | bytes 393232 | tf_op jit(solution)/shard_map/reduce_scatter | solution.py:29
  153.3 1.1 divide_convert_fusion
  154.6 7.9 %collective-permute-done = bf16[128,768]{1,0:T(8,128)(2,1)S(1)} collective-permute-done((bf16[128,768]{1,0:T(8,128)(2,1)S(1)}, bf16[128,768]{1,0:T(8,128)(2,1)S(1)}, u32[]{:S(2)}, u32[]{:S(2)}) %collective-permute-start) | collective-permute-done | bytes 196640 | tf_op jit(solution)/shard_map/ppermute | solution.py:62
  162.5 7.6 %collective-permute-done.1 = bf16[128,768]{1,0:T(8,128)(2,1)} collective-permute-done((bf16[128,768]{1,0:T(8,128)(2,1)S(1)}, bf16[128,768]{1,0:T(8,128)(2,1)}, u32[]{:S(2)}, u32[]{:S(2)}) %collective-permute-start.1) | collective-permute-done | bytes 196640 | tf_op jit(solution)/shard_map/ppermute | solution.py:62
  170.1 1.9 %maximum_multiply_fusion = f32[2]{0:T(128)} fusion(f32[1]{0:T(128)} %get-tuple-element.6, f32[1]{0:T(128)} %get-tuple-element.7), kind=kLoop, calls=%fused_computation.38 | loop fusion | flops 4 | bytes 16 | tf_op jit(solution)/shard_map/div | solution.py:70
  172.9 4.9 %collective-permute-done.2 = bf16[128,768]{1,0:T(8,128)(2,1)S(1)} collective-permute-done((bf16[128,768]{1,0:T(8,128)(2,1)}, bf16[128,768]{1,0:T(8,128)(2,1)S(1)}, u32[]{:S(2)}, u32[]{:S(2)}) %collective-permute-start.2) | collective-permute-done | bytes 196640 | tf_op jit(solution)/shard_map/ppermute | solution.py:62
  177.8 0.9 constant_dynamic-update-slice_fusion.6
  (37 shorter events, 5.3 us)
Async XLA Ops:
  7.2 43.7 %reduce-scatter.3.cloned.1.call-start = ((), (), s32[]{:S(2)}) async-start(), calls=%async_computation.2 | async-start | bytes 1966080 | tf_op jit(solution)/shard_map/reduce_scatter | solution.py:29
  7.2 5.3 %copy-start.5 = (u32[32]{0:T(128)S(1)}, u32[32]{0:T(128)}, u32[]{:S(2)}) copy-start(u32[32]{0:T(128)} %constant.64) | copy-start | bytes 388
  7.2 6.6 %copy-start.3 = (s32[2048]{0:T(1024)S(1)}, s32[2048]{0:T(1024)}, u32[]{:S(2)}) copy-start(s32[2048]{0:T(1024)} %param.6) | copy-start | bytes 24580
  7.3 6.6 %copy-start.4 = (s32[2048]{0:T(1024)S(1)}, s32[2048]{0:T(1024)}, u32[]{:S(2)}) copy-start(s32[2048]{0:T(1024)} %param.7) | copy-start | bytes 24580
  12.5 85.7 %all-gather.2.cloned.1.call-start = ((), (), s32[]{:S(2)}) async-start(), calls=%async_computation.3 | async-start | bytes 3342336 | tf_op jit(solution)/shard_map/all_gather | solution.py:51
  52.8 100.5 %reduce-scatter.5.cloned.1.call-start = ((), (), s32[]{:S(2)}) async-start(), calls=%async_computation.4 | async-start | bytes 1966080 | tf_op jit(solution)/shard_map/reduce_scatter | solution.py:29
  114.0 1.7 copy-start.1
  121.8 4.4 %copy-start = (bf16[2048,768]{1,0:T(8,128)(2,1)S(1)}, bf16[2048,768]{1,0:T(8,128)(2,1)}, u32[]{:S(2)}) copy-start(bf16[2048,768]{1,0:T(8,128)(2,1)} %param.5) | copy-start | bytes 9437188
  121.8 4.4 %copy-start.2 = (bf16[512,768]{1,0:T(8,128)(2,1)S(1)}, bf16[512,768]{1,0:T(8,128)(2,1)}, u32[]{:S(2)}) copy-start(bf16[512,768]{1,0:T(8,128)(2,1)} %param.8) | copy-start | bytes 2359300
  154.4 8.1 %collective-permute-start = (bf16[128,768]{1,0:T(8,128)(2,1)S(1)}, bf16[128,768]{1,0:T(8,128)(2,1)S(1)}, u32[]{:S(2)}, u32[]{:S(2)}) collective-permute-start(bf16[128,768]{1,0:T(8,128)(2,1)S(1)} %divide_convert_fusion), channel_id=1, source_target_pairs={{0,4},{4,8},{8,12},{12,0},{1,5},{5,9},{9,13},{13,1},{2,6},{6,10},{... | collective-permute-start | bytes 589832 | tf_op jit(solution)/shard_map/ppermute | solution.py:62
  162.5 7.6 %collective-permute-start.1 = (bf16[128,768]{1,0:T(8,128)(2,1)S(1)}, bf16[128,768]{1,0:T(8,128)(2,1)}, u32[]{:S(2)}, u32[]{:S(2)}) collective-permute-start(bf16[128,768]{1,0:T(8,128)(2,1)S(1)} %collective-permute-done), channel_id=1, source_target_pairs={{0,4},{4,8},{8,12},{12,0},{1,5},{5,9},{9,13},{13,1},{2,6},{6,10},{... | collective-permute-start | bytes 589832 | tf_op jit(solution)/shard_map/ppermute | solution.py:62
  170.1 7.7 %collective-permute-start.2 = (bf16[128,768]{1,0:T(8,128)(2,1)}, bf16[128,768]{1,0:T(8,128)(2,1)S(1)}, u32[]{:S(2)}, u32[]{:S(2)}) collective-permute-start(bf16[128,768]{1,0:T(8,128)(2,1)} %collective-permute-done.1), channel_id=1, source_target_pairs={{0,4},{4,8},{8,12},{12,0},{1,5},{5,9},{9,13},{13,1},{2,6},{6,10},{... | collective-permute-start | bytes 589832 | tf_op jit(solution)/shard_map/ppermute | solution.py:62
Sparse Core Ops, SparseCore 0:
  12.6 38.2 reduce-scatter.2
  53.8 44.3 all-gather.1
  119.2 34.0 reduce-scatter.4
